TPU v7x, 128 devices: a whole 4x4x4 slice. The times are simulated.
128 devices in a mesh: mod: 2 (over y_hi), exp: 64 (over z, y_lo, x, core).
Axes of the slice: x: 4, y: 4 (y_hi: 2, y_lo: 2; y = y_hi * 2 + y_lo), z: 4, core: 2. Of those that a mesh axis runs over, the one named last changes fastest.
Arguments:
- tokens: bfloat16 [2, 32768, 1024], P('mod', 'exp'), may hold values from -60 to 60
- bottleneck: bfloat16 [256, 4, 1024], P('exp'), may hold values from -6 to 6
- clip_ids: int32 [2, 32768], P('mod', 'exp'), may hold values from 0 to 255, as said below
- expert_ids: int32 [2, 32768], P('mod', 'exp'), may hold values from 0 to 63, as said below
- slots: int32 [2, 32768], P('mod', 'exp'), may hold values from 0 to 31, as said below
- norm1_gain: bfloat16 [2, 1024], P('mod'), may hold values from 0.099609375 to 1.8984375
- attn_qkv: bfloat16 [2, 1024, 3072], P('mod'), may hold values from -2 to 2
- attn_out: bfloat16 [2, 1024, 1024], P('mod'), may hold values from -0.1875 to 0.1875
- norm2_gain: bfloat16 [2, 1024], P('mod'), may hold values from 0.099609375 to 1.8984375
- router: bfloat16 [1024, 64], replicated, may hold values from -0.1875 to 0.1875
- fc_in: bfloat16 [64, 1024, 4096], P('exp'), may hold values from -0.1875 to 0.1875
- fc_out: bfloat16 [64, 4096, 1024], P('exp'), may hold values from -0.09375 to 0.09375
Outputs:
- mixed_tokens: bfloat16 [2, 32768, 1024], P('mod', 'exp')
- new_bottleneck: bfloat16 [256, 4, 1024], P('exp')
Inputs may be any that keep to these rules, and one draw needn't show every extreme that they name: `clip_ids`: Non-decreasing in each modality; the tokens of block b of 512 rows belong to clips b * 4 to (b + 1) * 4 - 1, each of which has one or more of them. `expert_ids`: each token's single expert. For the k tokens of one block of 512 rows of one modality that share an expert, the slots are 0 to k - 1 in some order; k is at most 32; in every block of each modality one expert, the same for all blocks of that modality, has k = 32.
All inputs are finite; a program needn't handle non-finite values.
Results may differ from a plain program's by a relative error of at most 0.0085.
Values may be sent and summed in bfloat16 or wider, within the bound.
A program may use at most 128 MiB of HBM per device.

v0:
```python
import math

import jax
import jax.numpy as jnp
from jax import lax
from jax.sharding import PartitionSpec as P

HEAD = 64
CAP_FACTOR = 2


EPSILON = 1e-06


def total_of_pieces(x, axis):
    blocks = lax.all_gather(x, axis).astype(jnp.float32)
    return blocks.sum(axis=0)


def layer_norm(features, scales):
    row_mean = jnp.mean(features, axis=-1, keepdims=True)
    centred = features - row_mean
    spread = jnp.mean(centred * centred, axis=-1, keepdims=True)
    return centred * lax.rsqrt(spread + EPSILON) * scales.astype(jnp.float32)


def attend(token_rows, latent_rows, token_clip, clip_start, scales, w_qkv, w_out):
    n_clips, n_latent, model_width = latent_rows.shape
    n_tokens = token_rows.shape[0]
    all_rows = jnp.concatenate(
        [token_rows, latent_rows.reshape(n_clips * n_latent, model_width)], axis=0
    )
    row_count = all_rows.shape[0]
    head_count = model_width // HEAD
    normed = layer_norm(all_rows.astype(jnp.float32), scales).astype(jnp.bfloat16)
    packed = jnp.dot(normed, w_qkv, preferred_element_type=jnp.float32).astype(jnp.bfloat16)
    queries = packed[:, :model_width].reshape(row_count, head_count, HEAD)
    key_rows = packed[:, model_width : 2 * model_width].reshape(row_count, head_count, HEAD)
    value_rows = packed[:, 2 * model_width :].reshape(row_count, head_count, HEAD)
    latent_clip = clip_start + jnp.arange(n_clips * n_latent, dtype=jnp.int32) // n_latent
    row_clip = jnp.concatenate([token_clip, latent_clip])
    allowed = row_clip[:, None] == row_clip[None, :]
    scores = jnp.einsum("qhd,khd->hqk", queries, key_rows, preferred_element_type=jnp.float32) * (
        1.0 / math.sqrt(HEAD)
    )
    scores = jnp.where(allowed[None, :, :], scores, -jnp.inf)
    row_max = jnp.max(scores, axis=-1, keepdims=True)
    weights = jnp.exp(scores - row_max)
    attn_weights = (weights / jnp.sum(weights, axis=-1, keepdims=True)).astype(jnp.bfloat16)
    attended = jnp.einsum(
        "hqk,khd->qhd", attn_weights, value_rows, preferred_element_type=jnp.float32
    )
    attended = attended.reshape(row_count, model_width).astype(jnp.bfloat16)
    updated = all_rows.astype(jnp.float32) + jnp.dot(
        attended, w_out, preferred_element_type=jnp.float32
    )
    return (updated[:n_tokens], updated[n_tokens:].reshape(n_clips, n_latent, model_width))


def apply_experts(received, weight_in, weight_out):
    local_count = weight_in.shape[0]
    row_count, slot_count, model_width = received.shape
    grouped = received.reshape(row_count // local_count, local_count, slot_count, model_width)
    hidden_units = jnp.einsum(
        "secd,edf->secf", grouped, weight_in, preferred_element_type=jnp.float32
    )
    activated = jax.nn.gelu(hidden_units, approximate=False).astype(jnp.bfloat16)
    outputs = jnp.einsum(
        "secf,efd->secd", activated, weight_out, preferred_element_type=jnp.float32
    )
    return outputs.astype(jnp.bfloat16).reshape(row_count, slot_count, model_width)


def mixture(mid_tokens, chosen, slot_ids, scales, router, fc_in, fc_out):
    model_width = mid_tokens.shape[1]
    expert_count = router.shape[1]
    capacity = CAP_FACTOR * mid_tokens.shape[0] // expert_count
    slot_total = expert_count * capacity
    expert_in = layer_norm(mid_tokens, scales).astype(jnp.bfloat16)
    logits = jnp.dot(expert_in, router, preferred_element_type=jnp.float32)
    column = jnp.arange(expert_count, dtype=jnp.int32)
    picked = jnp.sum(
        jnp.where(column[None, :] == chosen[:, None], logits, jnp.zeros_like(logits)), axis=1
    )
    gate_value = jax.nn.sigmoid(picked)
    served = slot_ids < capacity
    position = jnp.where(served, chosen * capacity + slot_ids, slot_total)
    buffer = (
        jnp.zeros((slot_total, model_width), jnp.bfloat16).at[position].set(expert_in, mode="drop")
    )
    buffer = buffer.reshape(expert_count, capacity, model_width)
    results = lax.all_to_all(
        apply_experts(
            lax.all_to_all(buffer, "exp", split_axis=0, concat_axis=0, tiled=True), fc_in, fc_out
        ),
        "exp",
        split_axis=0,
        concat_axis=0,
        tiled=True,
    )
    returned = jnp.take(
        results.reshape(slot_total, model_width), position, axis=0, mode="fill", fill_value=0
    )
    return (mid_tokens + gate_value[:, None] * returned.astype(jnp.float32)).astype(jnp.bfloat16)


def average_latent(mid_latent):
    summed = total_of_pieces(mid_latent.astype(jnp.bfloat16), "mod").astype(jnp.float32)
    return (summed * 0.5).astype(jnp.bfloat16)


def on_device(
    tokens,
    bottleneck,
    clip_ids,
    expert_ids,
    slots,
    norm1_gain,
    attn_qkv,
    attn_out,
    norm2_gain,
    router,
    fc_in,
    fc_out,
):
    clip_start = lax.axis_index("exp") * bottleneck.shape[0]
    mid_tokens, mid_latent = attend(
        tokens[0], bottleneck, clip_ids[0], clip_start, norm1_gain[0], attn_qkv[0], attn_out[0]
    )
    new_bottleneck = average_latent(mid_latent)
    mixed_tokens = mixture(
        mid_tokens, expert_ids[0], slots[0], norm2_gain[0], router, fc_in, fc_out
    )
    return (mixed_tokens[None], new_bottleneck)


def solution(mesh):
    in_specs = (
        P("mod", "exp", None),
        P("exp", None, None),
        P("mod", "exp"),
        P("mod", "exp"),
        P("mod", "exp"),
        P("mod", None),
        P("mod", None, None),
        P("mod", None, None),
        P("mod", None),
        P(),
        P("exp", None, None),
        P("exp", None, None),
    )
    out_specs = (P("mod", "exp", None), P("exp", None, None))
    return jax.shard_map(
        on_device, mesh=mesh, in_specs=in_specs, out_specs=out_specs, check_vma=False
    )
```

profile of v0, /device:TPU:74, one launch (start us, length us, event | category | flops | bytes accessed | tf_op | source)
XLA Modules:
  0.0 188.4 jit_solution(2352179801633982790)
XLA Ops:
  0.6 0.0 copy-start
  0.7 0.9 reshape.173
  1.6 1.5 convert_reduce_fusion
  3.0 1.7 fusion.39
  4.7 0.7 mul.153
  5.4 6.7 %fusion.34 = bf16[528,3072]{1,0:T(8,128)(2,1)S(1)} fusion(bf16[1,1024,3072]{2,1,0:T(8,128)(2,1)} %param.18, f32[1024]{0:T(1024)S(1)} %bitcast.162, f32[528]{0:T(1024)S(1)} %add_rsqrt_fusion, f32[528]{0:T(1024)S(1)} %broadcast_multiply_fusion, bf16[16,1024]{1,0:T(8,128)(2,1)S(1)} %reshape.173, bf16[512,1024]{1,0:T(8,128)(2,1)} %bitcast.150), kind=kOutput, calls=%fused_computation.40 | convolution fusion | flops 3327836160 | bytes 10625152 | tf_op jit(solution)/shard_map/dot_general | solution.py:36
  12.1 0.0 copy-start.8
  12.2 1.7 fusion.98
  13.8 2.4 %copy.23 = bf16[528,1024]{0,1:T(8,128)(2,1)} copy(bf16[528,1024]{1,0:T(8,128)(2,1)} %get-tuple-element.3) | data formatting | bytes 2162688 | tf_op jit(solution)/shard_map/slice | solution.py:37
  16.2 2.4 %copy.24 = bf16[528,1024]{0,1:T(8,128)(2,1)} copy(bf16[528,1024]{1,0:T(8,128)(2,1)} %get-tuple-element.2) | data formatting | bytes 2162688 | tf_op jit(solution)/shard_map/slice | solution.py:38
  18.6 0.0 copy-done.8
  18.6 1.0 broadcast_compare_fusion
  19.6 1.5 copy.22
  21.1 0.0 copy-start.4
  21.1 12.8 %fusion.99 = (f32[16,528]{1,0:T(8,128)S(1)}, f32[16,528,528]{1,2,0:T(8,128)}) fusion(pred[528,528]{0,1:T(8,128)(4,1)} %broadcast_compare_fusion, bf16[528,16,64]{0,2,1:T(8,128)(2,1)} %bitcast.152, bf16[528,16,64]{0,2,1:T(8,128)(2,1)} %bitcast.153), kind=kOutput, calls=%fused_computation.122 | convolution fusion | flops 588792320 | bytes 20317440 | tf_op jit(solution)/shard_map/sub | solution.py:48
  33.9 0.0 copy-done.4
  33.9 0.0 copy-start.3
  33.9 9.4 %fusion.51 = bf16[16,64,528]{2,1,0:T(8,128)(2,1)S(1)} fusion(bf16[528,16,64]{0,2,1:T(8,128)(2,1)S(1)} %bitcast.154, f32[16,528,528]{1,2,0:T(8,128)} %get-tuple-element.6, f32[16,528]{1,0:T(8,128)S(1)} %get-tuple-element.5), kind=kOutput, calls=%fused_computation.56 | convolution fusion | flops 580411392 | bytes 20038656 | tf_op jit(solution)/shard_map/hqk,khd->qhd/dot_general | solution.py:50
  43.3 0.0 copy-done
  43.3 0.0 copy-done.3
  43.3 0.0 copy-start.7
  43.3 0.0 copy-start.5
  43.4 0.0 copy-start.6
  43.4 1.4 convert_add_fusion
  44.7 0.0 copy-start.2
  44.7 0.2 slice_reduce_fusion
  44.9 1.2 copy-done.2
  46.1 0.3 multiply_reduce_fusion
  46.4 0.0 copy-done.7
  46.5 0.0 copy-done.5
  46.5 0.0 copy-done.6
  46.5 4.4 %scatter_custom_fusion = bf16[1024,1024]{1,0:T(8,128)(2,1)S(1)} fusion(s32[512]{0:T(512)S(1)} %bitcast.157, bf16[]{:T(256)} %constant.26.clone.1, f32[528,1024]{1,0:T(8,128)} %copy-done.2, f32[1024]{0:T(1024)S(1)} %bitcast.155, f32[512]{0:T(512)S(1)} %add_rsqrt_fusion.1, f32[512]{0:T(512)S(1)} %broadcast_multiply_fusion.1), kind=kCustom, calls=%fused_computation.65 | custom fusion | flops 2097152 | bytes 4203008 | tf_op jit(solution)/shard_map/scatter | solution.py:89
  50.9 34.9 %all_to_all.10 = bf16[64,16,1024]{2,1,0:T(8,128)(2,1)S(1)} all-to-all(bf16[64,16,1024]{2,1,0:T(8,128)(2,1)S(1)} %bitcast.147), channel_id=1, replica_groups=mesh['mod'=2,'exp'=64] {'exp'}, dimensions={0} | all-to-all | bytes 4194304 | tf_op jit(solution)/shard_map/all_to_all | solution.py:94
  85.9 44.9 %fusion.118 = bf16[64,16,4096]{2,1,0:T(8,128)(2,1)S(1)} fusion(bf16[64,16,1024]{2,1,0:T(8,128)(2,1)S(1)} %all_to_all.10, bf16[1,1024,4096]{2,1,0:T(8,128)(2,1)} %param.22), kind=kOutput, calls=%fused_computation.33.clone.clone.clone.1 | convolution fusion | flops 8862564352 | bytes 18874368 | tf_op jit(solution)/shard_map/secd,edf->secf/dot_general | solution.py:64
  130.7 0.0 copy-start.9
  130.8 12.3 %fusion.44 = bf16[64,16,1024]{2,1,0:T(8,128)(2,1)} fusion(bf16[1,4096,1024]{2,1,0:T(8,128)(2,1)} %param.23, bf16[64,16,4096]{2,1,0:T(8,128)(2,1)S(1)} %fusion.118), kind=kOutput, calls=%fused_computation.54 | convolution fusion | flops 8590983168 | bytes 18874368 | tf_op jit(solution)/shard_map/secf,efd->secd/dot_general | solution.py:68
  143.0 8.4 %all-to-all-start.1 = ((bf16[64,16,1024]{2,1,0:T(8,128)(2,1)}), bf16[64,16,1024]{2,1,0:T(8,128)(2,1)}, u32[]{:S(2)}, u32[]{:S(2)}) async-start(bf16[64,16,1024]{2,1,0:T(8,128)(2,1)} %fusion.44), calls=%async_computation.1 | async-start | bytes 4194304 | tf_op jit(solution)/shard_map/all_to_all | solution.py:92
  151.4 0.8 slice.35
  152.3 25.6 %all_gather.4 = bf16[2,4,4,1024]{3,2,1,0:T(4,128)(2,1)S(1)} all-gather(bf16[1,4,4,1024]{3,2,1,0:T(4,128)(2,1)S(1)} %convert_element_type.73), channel_id=1, replica_groups=mesh['mod'=2,'exp'=64] {'mod'}, dimensions={0}, use_global_device_ids=true | all-gather | bytes 98304 | tf_op jit(solution)/shard_map/all_gather | solution.py:16
  177.9 0.0 copy-done.9
  177.9 2.2 %fusion.56 = f32[512]{0:T(512)S(1)} fusion(bf16[1024,64]{0,1:T(8,128)(2,1)S(1)} %copy-done.9, s32[512]{0:T(512)S(1)} %bitcast.160, f32[528,1024]{1,0:T(8,128)} %copy-done.2, f32[1024]{0:T(1024)S(1)} %bitcast.156, f32[512]{0:T(512)S(1)} %add_rsqrt_fusion.1, f32[512]{0:T(512)S(1)} %broadcast_multiply_fusion.1), kind=kOutput, calls=%fused_computation.59 | convolution fusion | flops 69303808 | bytes 2240512 | tf_op jit(solution)/shard_map/dot_general | solution.py:80
  180.1 0.6 multiply_convert_fusion.1
  180.7 0.0 all-to-all-done.1
  180.7 0.0 copy-start.1
  180.7 4.7 %gather_fusion = bf16[512,1024]{1,0:T(8,128)(2,1)S(1)} fusion(bf16[1024,1024]{1,0:T(8,128)(2,1)} %bitcast.29, s32[1024]{0:T(1024)S(1)} %pad_clamp_fusion), kind=kCustom, calls=%fused_computation | custom fusion | bytes 2099200 | tf_op jit(solution)/shard_map/jit(_take)/gather | solution.py:101
  185.5 2.9 %fusion.61 = bf16[1,512,1024]{2,1,0:T(8,128)(2,1)} fusion(f32[528,1024]{1,0:T(8,128)} %copy-done.2, bf16[512,1024]{1,0:T(8,128)(2,1)S(1)} %gather_fusion, f32[512]{0:T(512)S(1)} %add_divide_fusion, pred[512]{0:T(512)(128)(4,1)S(1)} %compare_and_fusion), kind=kLoop, calls=%fused_computation.64 | loop fusion | flops 2621440 | bytes 4196864 | tf_op jit(solution)/shard_map/broadcast_in_dim | solution.py:134
  188.4 0.0 copy-done.1
  (13 shorter events, 0.1 us)
Async XLA Ops:
  0.6 42.7 %copy-start = (bf16[1,1024,1024]{2,1,0:T(8,128)(2,1)S(1)}, bf16[1,1024,1024]{2,1,0:T(8,128)(2,1)}, u32[]{:S(2)}) copy-start(bf16[1,1024,1024]{2,1,0:T(8,128)(2,1)} %param.19) | copy-start | bytes 6291460
  12.1 6.5 %copy-start.8 = (s32[1,512]{1,0:T(1,128)S(1)}, s32[1,512]{1,0:T(1,128)}, u32[]{:S(2)}) copy-start(s32[1,512]{1,0:T(1,128)} %param.14) | copy-start | bytes 6148
  21.1 12.8 %copy-start.4 = (bf16[528,1024]{0,1:T(8,128)(2,1)S(1)}, bf16[528,1024]{0,1:T(8,128)(2,1)}, u32[]{:S(2)}) copy-start(bf16[528,1024]{0,1:T(8,128)(2,1)} %copy.22) | copy-start | bytes 3244036
  33.9 9.4 %copy-start.3 = (bf16[1,512,1024]{2,1,0:T(8,128)(2,1)S(1)}, bf16[1,512,1024]{2,1,0:T(8,128)(2,1)}, u32[]{:S(2)}) copy-start(bf16[1,512,1024]{2,1,0:T(8,128)(2,1)} %param.12) | copy-start | bytes 3145732
  43.3 3.1 %copy-start.7 = (bf16[1,1024]{1,0:T(2,128)(2,1)S(1)}, bf16[1,1024]{1,0:T(2,128)(2,1)}, u32[]{:S(2)}) copy-start(bf16[1,1024]{1,0:T(2,128)(2,1)} %param.20) | copy-start | bytes 6148
  43.3 3.1 %copy-start.5 = (s32[1,512]{1,0:T(1,128)S(1)}, s32[1,512]{1,0:T(1,128)}, u32[]{:S(2)}) copy-start(s32[1,512]{1,0:T(1,128)} %param.16) | copy-start | bytes 6148
  43.4 3.1 %copy-start.6 = (s32[1,512]{1,0:T(1,128)S(1)}, s32[1,512]{1,0:T(1,128)}, u32[]{:S(2)}) copy-start(s32[1,512]{1,0:T(1,128)} %param.15) | copy-start | bytes 6148
  44.7 1.4 copy-start.2
  130.7 47.1 %copy-start.9 = (bf16[1024,64]{0,1:T(8,128)(2,1)S(1)}, bf16[1024,64]{0,1:T(8,128)(2,1)}, u32[]{:S(2)}) copy-start(bf16[1024,64]{0,1:T(8,128)(2,1)} %param.21) | copy-start | bytes 393220
  143.0 37.7 %all-to-all-start.1 = ((bf16[64,16,1024]{2,1,0:T(8,128)(2,1)}), bf16[64,16,1024]{2,1,0:T(8,128)(2,1)}, u32[]{:S(2)}, u32[]{:S(2)}) async-start(bf16[64,16,1024]{2,1,0:T(8,128)(2,1)} %fusion.44), calls=%async_computation.1 | async-start | bytes 4194304 | tf_op jit(solution)/shard_map/all_to_all | solution.py:92
  180.7 7.7 %copy-start.1 = (bf16[1,1024,1024]{2,1,0:T(8,128)(2,1)S(1)}, bf16[1,1024,1024]{2,1,0:T(8,128)(2,1)}, u32[]{:S(2)}) copy-start(bf16[1,1024,1024]{2,1,0:T(8,128)(2,1)} %param.19) | copy-start | bytes 6291460
where the time goes:
time: 191 us; the launch traced here: 188 us
  matrix products  89.6 us (47%)
  blocking collectives  60.5 us (32%)
  local copies, waits for them, and re-layouts  15.7 us (8%)
  other arithmetic  13.5 us (7%)
  starting transfers between devices  8.37 us (4%)
    dot_general x1, matrix products, apply_experts(): jnp.einsum('secd,edf->secf', grouped, weight_in, preferred_element_type=j...  44.9 us
    all_to_all x1, blocking collectives, mixture(): lax.all_to_all(buffer, 'exp', split_axis=0, concat_axis=0, tiled=True)  34.9 us
    all_gather x1, blocking collectives, total_of_pieces(): blocks = lax.all_gather(x, axis).astype(jnp.float32)  25.6 us
    sub x1, matrix products, attend(): weights = jnp.exp(scores - row_max)  12.8 us
    dot_general x1, matrix products, apply_experts(): jnp.einsum('secf,efd->secd', activated, weight_out, preferred_element_typ...  12.3 us
    dot_general x1, matrix products, attend(): jnp.einsum('hqk,khd->qhd', attn_weights, value_rows, preferred_element_ty...  9.41 us
    all_to_all x1, starting transfers between devices, mixture(): lax.all_to_all(apply_experts(lax.all_to_all(buffer, 'exp', split_axis=0,...  8.37 us
    dot_general x1, matrix products, attend(): jnp.dot(normed, w_qkv, preferred_element_type=jnp.float32)  6.74 us
  transfers between devices with their start and end apart: 1, of which 0 were waited for; matrix products, arithmetic and copies ran while one was open for 2% of the time, Pallas kernels for 0%

commit v1 on v0

v1 whole, which is shorter than its diff:
```python
import functools
import math

import jax
import jax.numpy as jnp
from jax import lax
from jax.experimental import pallas as pl
from jax.experimental.pallas import tpu as pltpu
from jax.sharding import PartitionSpec as P

MESH = pl.DeviceIdType.MESH
EPSILON = 1e-06
BIG = 2.0**100
F32 = jnp.float32
BF16 = jnp.bfloat16

T = 512
L = 16
R = T + L
KEYS = 640
D = 1024
FF = 4096
CAP = 16
EXPERTS = 64
GROUPS = 4
ORDER = (2, 1, 3, 0)
FF_TILE = 512


def dot(a, b):
    return lax.dot_general(a, b, (((1,), (0,)), ((), ())), preferred_element_type=F32)


def dot_nt(a, b):
    return lax.dot_general(a, b, (((1,), (1,)), ((), ())), preferred_element_type=F32)


def norm_rows(rows, gain):
    mean = jnp.mean(rows, axis=-1, keepdims=True)
    centred = rows - mean
    spread = jnp.mean(centred * centred, axis=-1, keepdims=True)
    return centred * lax.rsqrt(spread + EPSILON) * gain


def column_of(row):
    eye = lax.broadcasted_iota(jnp.int32, (128, 128), 0) == lax.broadcasted_iota(
        jnp.int32, (128, 128), 1
    )
    pieces = []
    for i in range(row.shape[1] // 128):
        block = jnp.broadcast_to(row[:, i * 128 : (i + 1) * 128], (128, 128))
        pieces.append(jnp.sum(jnp.where(eye, block, 0.0), axis=1, keepdims=True))
    return jnp.concatenate(pieces, axis=0)


def layer_kernel(
    tok, lat, clip, eid, slot, g1, g2, router, wqkv_hbm, wout_hbm, fin_hbm, fout_hbm,
    out, newb,
    wqkv, wout, fin, fout, latx, normed, packed, qmask, kmask, attended, mid, expert_in,
    gate, disp, recv, outb, ret, acc, lat_send, lat_recv,
    wsem, dsend, drecv, rsend, rrecv, lsem,
):
    m = lax.axis_index("mod")
    e = lax.axis_index("exp")
    me = lax.rem(e, 16)
    z = e // 16
    y = me // 8
    x = lax.rem(me // 2, 4)
    c = lax.rem(me, 2)

    def partner(r):
        return (
            lax.rem(y + r // 8, 2) * 8
            + lax.rem(x + lax.rem(r // 2, 4), 4) * 2
            + lax.rem(c + r, 2)
        )

    qkv_copies = []
    for i in range(3):
        cols = pl.ds(i * D, D)
        cp = pltpu.make_async_copy(wqkv_hbm.at[0, :, cols], wqkv.at[:, cols], wsem.at[i])
        cp.start()
        qkv_copies.append(cp)
    out_copy = pltpu.make_async_copy(wout_hbm.at[0], wout, wsem.at[3])
    fin_copy = pltpu.make_async_copy(fin_hbm.at[0], fin, wsem.at[4])
    fout_copy = pltpu.make_async_copy(fout_hbm.at[0], fout, wsem.at[5])

    barrier = pltpu.get_barrier_semaphore()
    pl.semaphore_signal(barrier, inc=1, device_id=(1 - m, e), device_id_type=MESH)
    for g in range(GROUPS):
        zz = lax.rem(z + g, 4) * 16

        def greet(r, carry, zz=zz):
            pl.semaphore_signal(
                barrier, inc=1, device_id=(m, zz + partner(r)), device_id_type=MESH
            )
            return carry

        lax.fori_loop(1 if g == 0 else 0, 16, greet, 0)

    clip_start = e * 4
    lane = lax.broadcasted_iota(jnp.int32, (T, 128), 1)
    clip_col = column_of((clip[...] - clip_start).astype(F32)).astype(jnp.int32)
    hit = lane == clip_col
    qmask[0:T, :] = jnp.where(hit | (lane == 4), -BIG, 0.0).astype(BF16)
    kmask[0:T, :] = jnp.where(hit | (lane >= 4), 0.0, 1.0).astype(BF16)
    lane_l = lax.broadcasted_iota(jnp.int32, (L, 128), 1)
    clip_l = lax.broadcasted_iota(jnp.int32, (L, 128), 0) // 4
    hit_l = lane_l == clip_l
    qmask[T:R, :] = jnp.where(hit_l | (lane_l == 4), -BIG, 0.0).astype(BF16)
    kmask[T:R, :] = jnp.where(hit_l | (lane_l >= 4), 0.0, 1.0).astype(BF16)
    lane_p = lax.broadcasted_iota(jnp.int32, (KEYS - R, 128), 1)
    kmask[R:KEYS, :] = jnp.where(lane_p == 4, 1.0, 0.0).astype(BF16)
    packed[R:KEYS, :] = jnp.zeros((KEYS - R, 3 * D), BF16)

    gain1 = g1[...].astype(F32)

    def norm1(i, carry):
        rows = pl.ds(pl.multiple_of(i * 32, 32), 32)
        normed[rows, :] = norm_rows(tok[0, rows, :].astype(F32), gain1).astype(BF16)
        return carry

    lax.fori_loop(0, T // 32, norm1, 0)
    for i in range(4):
        latx[4 * i : 4 * i + 4, :] = lat[i].astype(F32)
    normed[T:R, :] = norm_rows(latx[...], gain1).astype(BF16)

    for i in range(3):
        qkv_copies[i].wait()
        if i == 0:
            out_copy.start()

        def project(j, carry, i=i):
            cols = pl.ds(pl.multiple_of(i * D + j * 512, 512), 512)
            piece = dot(normed[...], wqkv[:, cols]).astype(BF16)
            if i == 0:
                piece = piece * (1.0 / 8.0)
            packed[0:R, cols] = piece.astype(BF16)
            return carry

        lax.fori_loop(0, 2, project, 0)
    fin_copy.start()
    fout_copy.start()

    def pair(p, carry):
        col = pl.multiple_of(p * 128, 128)
        keys = jnp.concatenate([packed[:, pl.ds(D + col, 128)], kmask[...]], axis=1)
        values = jnp.concatenate(
            [packed[:, pl.ds(2 * D + col, 128)], jnp.ones((KEYS, 128), BF16)], axis=1
        )
        for row0 in range(0, R, 176):
            queries = packed[row0 : row0 + 176, pl.ds(col, 128)]
            first = lax.broadcasted_iota(jnp.int32, (176, 128), 1) < 64
            heads = []
            for half in range(2):
                mine = jnp.where(first if half == 0 else ~first, queries, jnp.zeros_like(queries))
                q = jnp.concatenate([mine, qmask[row0 : row0 + 176, :]], axis=1)
                s = dot_nt(q, keys)
                top = jnp.max(s, axis=-1, keepdims=True)
                w = jnp.exp(s - top).astype(BF16)
                o = dot(w, values)
                heads.append(o[:, :128] / o[:, 128:])
            attended[row0 : row0 + 176, pl.ds(col, 128)] = jnp.where(
                first, heads[0], heads[1]
            ).astype(BF16)
        return carry

    lax.fori_loop(0, D // 128, pair, 0)

    out_copy.wait()

    def project_out(j, carry):
        cols = pl.ds(pl.multiple_of(j * 512, 512), 512)
        mid[:, cols] = dot(attended[...], wout[:, cols])
        return carry

    lax.fori_loop(0, 2, project_out, 0)

    gain2 = g2[...].astype(F32)

    def norm2(i, carry):
        rows = pl.ds(pl.multiple_of(i * 32, 32), 32)
        updated = mid[rows, :] + tok[0, rows, :].astype(F32)
        mid[rows, :] = updated
        expert_in[rows, :] = norm_rows(updated, gain2).astype(BF16)
        return carry

    lax.fori_loop(0, T // 32, norm2, 0)
    lat_send[...] = (mid[T:R, :] + latx[...]).astype(BF16)

    pos_row = jnp.where(slot[...] < CAP, eid[...] * CAP + slot[...], -1)
    pl.semaphore_wait(barrier, 64)
    lat_copy = pltpu.make_async_remote_copy(
        src_ref=lat_send, dst_ref=lat_recv, send_sem=lsem.at[0], recv_sem=lsem.at[1],
        device_id=(1 - m, e), device_id_type=MESH,
    )
    lat_copy.start()
    for g in ORDER:
        zz = lax.rem(z + g, 4)
        place = lax.broadcasted_iota(jnp.int32, (256, T), 0) + zz * 256
        onehot = jnp.where(place == pos_row, 1.0, 0.0).astype(BF16)
        disp[g] = dot(onehot, expert_in[...]).astype(BF16).reshape(16, CAP, D)

        def send(r, carry, g=g, zz=zz):
            j = partner(r)
            pltpu.make_async_remote_copy(
                src_ref=disp.at[g, j], dst_ref=recv.at[g, me],
                send_sem=dsend.at[g], recv_sem=drecv.at[g],
                device_id=(m, zz * 16 + j), device_id_type=MESH,
            ).start()
            return carry

        lax.fori_loop(1 if g == 0 else 0, 16, send, 0)
    recv[0, me] = disp[0, me]

    logits = dot(expert_in[...], router[...])
    eid_col = column_of(eid[...].astype(F32)).astype(jnp.int32)
    expert_lane = lax.broadcasted_iota(jnp.int32, (T, EXPERTS), 1)
    picked = jnp.sum(jnp.where(expert_lane == eid_col, logits, 0.0), axis=1, keepdims=True)
    gate[...] = 1.0 / (1.0 + jnp.exp(-picked))
    pos_col = column_of(pos_row.astype(F32)).astype(jnp.int32)

    fin_copy.wait()
    fout_copy.wait()
    for g in ORDER:
        n = 15 if g == 0 else 16
        zz = lax.rem(z + 4 - g, 4)
        landed = recv.at[g, pl.ds(0, n)]
        pltpu.make_async_copy(landed, landed, drecv.at[g]).wait()
        rows_in = recv[g].reshape(256, D)
        acc[...] = jnp.zeros_like(acc)

        def expert(f, carry, rows_in=rows_in):
            cols = pl.ds(pl.multiple_of(f * FF_TILE, FF_TILE), FF_TILE)
            h = dot(rows_in, fin[:, cols])
            h = (0.5 * h * (1.0 + lax.erf(h * math.sqrt(0.5)))).astype(BF16)
            acc[...] += dot(h, fout[cols, :])
            return carry

        lax.fori_loop(0, FF // FF_TILE, expert, 0)
        outb[g] = acc[...].astype(BF16).reshape(16, CAP, D)

        def send_back(r, carry, g=g, zz=zz):
            j = partner(r)
            pltpu.make_async_remote_copy(
                src_ref=outb.at[g, j], dst_ref=ret.at[g, me],
                send_sem=rsend.at[g], recv_sem=rrecv.at[g],
                device_id=(m, zz * 16 + j), device_id_type=MESH,
            ).start()
            return carry

        lax.fori_loop(1 if g == 0 else 0, 16, send_back, 0)
        if g == 0:
            ret[0, me] = outb[0, me]

    lat_copy.wait()
    both = (lat_send[...].astype(F32) + lat_recv[...].astype(F32)) * 0.5
    for i in range(4):
        newb[i] = both[4 * i : 4 * i + 4, :].astype(BF16)

    for k, g in enumerate(ORDER):
        n = 15 if g == 0 else 16
        zz = lax.rem(z + g, 4)
        landed = ret.at[g, pl.ds(0, n)]
        pltpu.make_async_copy(landed, landed, rrecv.at[g]).wait()
        place = lax.broadcasted_iota(jnp.int32, (T, 256), 1) + zz * 256
        onehot = jnp.where(place == pos_col, 1.0, 0.0).astype(BF16)
        total = mid[0:T, :] + gate[...] * dot(onehot, ret[g].reshape(256, D))
        if k < GROUPS - 1:
            mid[0:T, :] = total
        else:
            out[0] = total.astype(BF16)

    for g in range(GROUPS):
        n = 15 if g == 0 else 16
        sent = disp.at[g, pl.ds(0, n)]
        pltpu.make_async_copy(sent, sent, dsend.at[g]).wait()
        sent = outb.at[g, pl.ds(0, n)]
        pltpu.make_async_copy(sent, sent, rsend.at[g]).wait()


def on_device(
    tokens, bottleneck, clip_ids, expert_ids, slots, norm1_gain, attn_qkv, attn_out,
    norm2_gain, router, fc_in, fc_out,
):
    vmem = pl.BlockSpec(memory_space=pltpu.VMEM)
    hbm = pl.BlockSpec(memory_space=pl.ANY)
    dma = pltpu.SemaphoreType.DMA
    return pl.pallas_call(
        layer_kernel,
        out_shape=(
            jax.ShapeDtypeStruct(tokens.shape, BF16),
            jax.ShapeDtypeStruct(bottleneck.shape, BF16),
        ),
        in_specs=[vmem] * 8 + [hbm] * 4,
        out_specs=(vmem, vmem),
        scratch_shapes=[
            pltpu.VMEM((D, 3 * D), BF16),
            pltpu.VMEM((D, D), BF16),
            pltpu.VMEM((D, FF), BF16),
            pltpu.VMEM((FF, D), BF16),
            pltpu.VMEM((L, D), F32),
            pltpu.VMEM((R, D), BF16),
            pltpu.VMEM((KEYS, 3 * D), BF16),
            pltpu.VMEM((R, 128), BF16),
            pltpu.VMEM((KEYS, 128), BF16),
            pltpu.VMEM((R, D), BF16),
            pltpu.VMEM((R, D), F32),
            pltpu.VMEM((T, D), BF16),
            pltpu.VMEM((T, 1), F32),
            pltpu.VMEM((GROUPS, 16, CAP, D), BF16),
            pltpu.VMEM((GROUPS, 16, CAP, D), BF16),
            pltpu.VMEM((GROUPS, 16, CAP, D), BF16),
            pltpu.VMEM((GROUPS, 16, CAP, D), BF16),
            pltpu.VMEM((256, D), F32),
            pltpu.VMEM((L, D), BF16),
            pltpu.VMEM((L, D), BF16),
            dma((6,)),
            dma((GROUPS,)),
            dma((GROUPS,)),
            dma((GROUPS,)),
            dma((GROUPS,)),
            dma((2,)),
        ],
        compiler_params=pltpu.CompilerParams(
            collective_id=0, has_side_effects=True, vmem_limit_bytes=62 * 2**20
        ),
    )(
        tokens, bottleneck, clip_ids, expert_ids, slots, norm1_gain, norm2_gain, router,
        attn_qkv, attn_out, fc_in, fc_out,
    )


def solution(mesh):
    in_specs = (
        P("mod", "exp", None),
        P("exp", None, None),
        P("mod", "exp"),
        P("mod", "exp"),
        P("mod", "exp"),
        P("mod", None),
        P("mod", None, None),
        P("mod", None, None),
        P("mod", None),
        P(),
        P("exp", None, None),
        P("exp", None, None),
    )
    out_specs = (P("mod", "exp", None), P("exp", None, None))
    return jax.shard_map(
        on_device, mesh=mesh, in_specs=in_specs, out_specs=out_specs, check_vma=False
    )
```

time: 191 us -> 115 us (0.60); the launches traced: 188 us -> 115 us
  Pallas kernels: 0 us -> 109 us
  matrix products: 89.6 us -> 0 us
  blocking collectives: 60.5 us -> 0 us
  other arithmetic: 13.5 us -> 0 us
  local copies, waits for them, and re-layouts: 15.7 us -> 5.39 us
  starting transfers between devices: 8.37 us -> 0 us
    pallas_call x0 -> x1, Pallas kernels: none -> 109 us  [on_device(): pl.pallas_call(layer_kernel, out_shape=(jax.ShapeDtypeStruct(tokens.shape...]
    dot_general x6 -> x0, matrix products: 76.8 us -> none  [the longest x1 44.9 us: apply_experts(): jnp.einsum('secd,edf->secf', grouped, weight_in, preferred_element_type=j...]
    all_to_all x1 -> x0, blocking collectives: 34.9 us -> none  [mixture(): lax.all_to_all(buffer, 'exp', split_axis=0, concat_axis=0, tiled=True)]
    all_gather x1 -> x0, blocking collectives: 25.6 us -> none  [total_of_pieces(): blocks = lax.all_gather(x, axis).astype(jnp.float32)]
    sub x1 -> x0, matrix products: 12.8 us -> none  [attend(): weights = jnp.exp(scores - row_max)]
    slice x5 -> x0, local copies, waits for them, and re-layouts: 8.8 us -> none  [the longest x2 4.06 us: attend(): packed[:, model_width:2 * model_width].reshape(row_count, head_count, HEAD)]
    all_to_all x1 -> x0, starting transfers between devices: 8.37 us -> none  [mixture(): lax.all_to_all(apply_experts(lax.all_to_all(buffer, 'exp', split_axis=0,...]
    gather x1 -> x0, local copies, waits for them, and re-layouts: 4.74 us -> none  [mixture(): jnp.take(results.reshape(slot_total, model_width), position, axis=0, mode...]
  transfers between devices with their start and end apart: 1 -> 0, of which waited for: 0 -> 0; matrix products, arithmetic and copies ran while one was open for 2% -> 0% of each run, Pallas kernels for 0% -> 0%
where the time goes in v1:
time: 115 us
  Pallas kernels  109 us (95%)
  local copies, waits for them, and re-layouts  5.39 us (5%)
    pallas_call x1, Pallas kernels, on_device(): pl.pallas_call(layer_kernel, out_shape=(jax.ShapeDtypeStruct(tokens.shape...  109 us
    unnamed x3, local copies, waits for them, and re-layouts  5.39 us

profile of v1, /device:TPU:74, one launch (start us, length us, event | category | flops | bytes accessed | tf_op | source)
XLA Modules:
  0.0 115.0 jit_solution(9759951202345041932)
XLA Ops:
  0.6 1.7 %copy.14.router = bf16[1024,64]{1,0:T(8,128)(2,1)} copy(bf16[1024,64]{0,1:T(8,128)(2,1)} %param.21) | data formatting | bytes 262144 | tf_op args[9]
  2.4 109.0 %shard_map.131 = (bf16[1,512,1024]{2,1,0:T(8,128)(2,1)}, bf16[4,4,1024]{2,1,0:T(4,128)(2,1)}) custom-call(bf16[1,512,1024]{2,1,0:T(8,128)(2,1)} %tok.1, bf16[4,4,1024]{2,1,0:T(4,128)(2,1)} %lat.1, s32[1,512]{1,0:T(1,128)} %clip.1, s32[1,512]{1,0:T(1,128)} %eid.1, s32[1,512]{1,0:T(1,128)} %slot.1, bf16[1,1024]{1,0:T(2,128)(2,1)} %g1.1, bf16[1,1024]{1,0:T(2,128)(2,1)} %g2.1, ...), custom_call_target="tpu_custom_call" | custom-call | tf_op jit(solution)/shard_map/pallas_call | solution.py:289
  111.3 2.3 %copy.17 = bf16[1,512,1024]{2,1,0:T(8,128)(2,1)} copy(bf16[1,512,1024]{2,1,0:T(8,128)(2,1)} %get-tuple-element.4) | data formatting | bytes 2097152
  113.6 1.4 %copy.18 = bf16[4,4,1024]{2,1,0:T(4,128)(2,1)} copy(bf16[4,4,1024]{2,1,0:T(4,128)(2,1)} %get-tuple-element.5) | data formatting | bytes 65536

commit v2 on v1

--- a/solution.py
+++ b/solution.py
@@ -23,7 +23,6 @@
 CAP = 16
 EXPERTS = 64
 GROUPS = 4
-ORDER = (2, 1, 3, 0)
 FF_TILE = 512
 
 
@@ -62,17 +61,25 @@
 ):
     m = lax.axis_index("mod")
     e = lax.axis_index("exp")
-    me = lax.rem(e, 16)
     z = e // 16
-    y = me // 8
-    x = lax.rem(me // 2, 4)
-    c = lax.rem(me, 2)
-
-    def partner(r):
-        return (
-            lax.rem(y + r // 8, 2) * 8
-            + lax.rem(x + lax.rem(r // 2, 4), 4) * 2
-            + lax.rem(c + r, 2)
+    y = lax.rem(e // 8, 2)
+    x = lax.rem(e // 2, 4)
+    c = lax.rem(e, 2)
+    me = z * 4 + y * 2 + c
+
+    def partner(j, r, sign):
+        oz = lax.rem(r, 4)
+        zz = lax.rem(z + 4 + sign * oz, 4)
+        xx = lax.rem(x + 8 + sign * (oz + j), 4)
+        yy = lax.rem(y + lax.rem(r // 4, 2), 2)
+        cc = lax.rem(c + r // 8, 2)
+        return zz * 4 + yy * 2 + cc, zz * 16 + yy * 8 + xx * 2 + cc
+
+    def places(i, j):
+        zz = i // 64
+        xx = lax.rem(x + 4 - z + zz + j, 4)
+        return (zz * 16 + lax.rem(i // 32, 2) * 8 + xx * 2 + lax.rem(i // 16, 2)) * CAP + lax.rem(
+            i, 16
         )
 
     qkv_copies = []
@@ -88,11 +95,10 @@
     barrier = pltpu.get_barrier_semaphore()
     pl.semaphore_signal(barrier, inc=1, device_id=(1 - m, e), device_id_type=MESH)
     for g in range(GROUPS):
-        zz = lax.rem(z + g, 4) * 16
-
-        def greet(r, carry, zz=zz):
+
+        def greet(r, carry, g=g):
             pl.semaphore_signal(
-                barrier, inc=1, device_id=(m, zz + partner(r)), device_id_type=MESH
+                barrier, inc=1, device_id=(m, partner(g, r, 1)[1]), device_id_type=MESH
             )
             return carry
 
@@ -116,11 +122,11 @@
     gain1 = g1[...].astype(F32)
 
     def norm1(i, carry):
-        rows = pl.ds(pl.multiple_of(i * 32, 32), 32)
+        rows = pl.ds(pl.multiple_of(i * 128, 128), 128)
         normed[rows, :] = norm_rows(tok[0, rows, :].astype(F32), gain1).astype(BF16)
         return carry
 
-    lax.fori_loop(0, T // 32, norm1, 0)
+    lax.fori_loop(0, T // 128, norm1, 0)
     for i in range(4):
         latx[4 * i : 4 * i + 4, :] = lat[i].astype(F32)
     normed[T:R, :] = norm_rows(latx[...], gain1).astype(BF16)
@@ -148,21 +154,18 @@
         values = jnp.concatenate(
             [packed[:, pl.ds(2 * D + col, 128)], jnp.ones((KEYS, 128), BF16)], axis=1
         )
-        for row0 in range(0, R, 176):
-            queries = packed[row0 : row0 + 176, pl.ds(col, 128)]
-            first = lax.broadcasted_iota(jnp.int32, (176, 128), 1) < 64
-            heads = []
-            for half in range(2):
-                mine = jnp.where(first if half == 0 else ~first, queries, jnp.zeros_like(queries))
-                q = jnp.concatenate([mine, qmask[row0 : row0 + 176, :]], axis=1)
-                s = dot_nt(q, keys)
-                top = jnp.max(s, axis=-1, keepdims=True)
-                w = jnp.exp(s - top).astype(BF16)
-                o = dot(w, values)
-                heads.append(o[:, :128] / o[:, 128:])
-            attended[row0 : row0 + 176, pl.ds(col, 128)] = jnp.where(
-                first, heads[0], heads[1]
-            ).astype(BF16)
+        queries = packed[0:R, pl.ds(col, 128)]
+        first = lax.broadcasted_iota(jnp.int32, (R, 128), 1) < 64
+        heads = []
+        for half in range(2):
+            mine = jnp.where(first if half == 0 else ~first, queries, jnp.zeros_like(queries))
+            q = jnp.concatenate([mine, qmask[...]], axis=1)
+            s = dot_nt(q, keys)
+            top = jnp.max(s, axis=-1, keepdims=True)
+            w = jnp.exp(s - top).astype(BF16)
+            o = dot(w, values)
+            heads.append(o[:, :128] / o[:, 128:])
+        attended[:, pl.ds(col, 128)] = jnp.where(first, heads[0], heads[1]).astype(BF16)
         return carry
 
     lax.fori_loop(0, D // 128, pair, 0)
@@ -179,13 +182,13 @@
     gain2 = g2[...].astype(F32)
 
     def norm2(i, carry):
-        rows = pl.ds(pl.multiple_of(i * 32, 32), 32)
+        rows = pl.ds(pl.multiple_of(i * 128, 128), 128)
         updated = mid[rows, :] + tok[0, rows, :].astype(F32)
         mid[rows, :] = updated
         expert_in[rows, :] = norm_rows(updated, gain2).astype(BF16)
         return carry
 
-    lax.fori_loop(0, T // 32, norm2, 0)
+    lax.fori_loop(0, T // 128, norm2, 0)
     lat_send[...] = (mid[T:R, :] + latx[...]).astype(BF16)
 
     pos_row = jnp.where(slot[...] < CAP, eid[...] * CAP + slot[...], -1)
@@ -195,18 +198,17 @@
         device_id=(1 - m, e), device_id_type=MESH,
     )
     lat_copy.start()
-    for g in ORDER:
-        zz = lax.rem(z + g, 4)
-        place = lax.broadcasted_iota(jnp.int32, (256, T), 0) + zz * 256
+    for g in range(GROUPS):
+        place = places(lax.broadcasted_iota(jnp.int32, (256, 1), 0), g)
         onehot = jnp.where(place == pos_row, 1.0, 0.0).astype(BF16)
         disp[g] = dot(onehot, expert_in[...]).astype(BF16).reshape(16, CAP, D)
 
-        def send(r, carry, g=g, zz=zz):
-            j = partner(r)
+        def send(r, carry, g=g):
+            j, there = partner(g, r, 1)
             pltpu.make_async_remote_copy(
                 src_ref=disp.at[g, j], dst_ref=recv.at[g, me],
                 send_sem=dsend.at[g], recv_sem=drecv.at[g],
-                device_id=(m, zz * 16 + j), device_id_type=MESH,
+                device_id=(m, there), device_id_type=MESH,
             ).start()
             return carry
 
@@ -222,9 +224,8 @@
 
     fin_copy.wait()
     fout_copy.wait()
-    for g in ORDER:
+    for g in range(GROUPS):
         n = 15 if g == 0 else 16
-        zz = lax.rem(z + 4 - g, 4)
         landed = recv.at[g, pl.ds(0, n)]
         pltpu.make_async_copy(landed, landed, drecv.at[g]).wait()
         rows_in = recv[g].reshape(256, D)
@@ -240,12 +241,12 @@
         lax.fori_loop(0, FF // FF_TILE, expert, 0)
         outb[g] = acc[...].astype(BF16).reshape(16, CAP, D)
 
-        def send_back(r, carry, g=g, zz=zz):
-            j = partner(r)
+        def send_back(r, carry, g=g):
+            j, there = partner(g, r, -1)
             pltpu.make_async_remote_copy(
                 src_ref=outb.at[g, j], dst_ref=ret.at[g, me],
                 send_sem=rsend.at[g], recv_sem=rrecv.at[g],
-                device_id=(m, zz * 16 + j), device_id_type=MESH,
+                device_id=(m, there), device_id_type=MESH,
             ).start()
             return carry
 
@@ -258,15 +259,14 @@
     for i in range(4):
         newb[i] = both[4 * i : 4 * i + 4, :].astype(BF16)
 
-    for k, g in enumerate(ORDER):
+    for g in range(GROUPS):
         n = 15 if g == 0 else 16
-        zz = lax.rem(z + g, 4)
         landed = ret.at[g, pl.ds(0, n)]
         pltpu.make_async_copy(landed, landed, rrecv.at[g]).wait()
-        place = lax.broadcasted_iota(jnp.int32, (T, 256), 1) + zz * 256
+        place = places(lax.broadcasted_iota(jnp.int32, (1, 256), 1), g)
         onehot = jnp.where(place == pos_col, 1.0, 0.0).astype(BF16)
         total = mid[0:T, :] + gate[...] * dot(onehot, ret[g].reshape(256, D))
-        if k < GROUPS - 1:
+        if g < GROUPS - 1:
             mid[0:T, :] = total
         else:
             out[0] = total.astype(BF16)

time: 115 us -> 100 us (0.87)
  the two profiles are of different devices: /device:TPU:74 before, /device:TPU:1 now
where the time goes in v2:
time: 100 us
  Pallas kernels  94 us (94%)
  local copies, waits for them, and re-layouts  5.39 us (5%)
    pallas_call x1, Pallas kernels, on_device(): pl.pallas_call(layer_kernel, out_shape=(jax.ShapeDtypeStruct(tokens.shape...  94 us
    unnamed x3, local copies, waits for them, and re-layouts  5.39 us

profile of v2, /device:TPU:1, one launch (start us, length us, event | category | flops | bytes accessed | tf_op | source)
XLA Modules:
  0.0 100.1 jit_solution(11144414097789075359)
XLA Ops:
  0.6 1.7 %copy.14.router = bf16[1024,64]{1,0:T(8,128)(2,1)} copy(bf16[1024,64]{0,1:T(8,128)(2,1)} %param.21) | data formatting | bytes 262144 | tf_op args[9]
  2.4 94.0 %shard_map.131 = (bf16[1,512,1024]{2,1,0:T(8,128)(2,1)}, bf16[4,4,1024]{2,1,0:T(4,128)(2,1)}) custom-call(bf16[1,512,1024]{2,1,0:T(8,128)(2,1)} %tok.1, bf16[4,4,1024]{2,1,0:T(4,128)(2,1)} %lat.1, s32[1,512]{1,0:T(1,128)} %clip.1, s32[1,512]{1,0:T(1,128)} %eid.1, s32[1,512]{1,0:T(1,128)} %slot.1, bf16[1,1024]{1,0:T(2,128)(2,1)} %g1.1, bf16[1,1024]{1,0:T(2,128)(2,1)} %g2.1, ...), custom_call_target="tpu_custom_call" | custom-call | tf_op jit(solution)/shard_map/pallas_call | solution.py:289
  96.4 2.3 %copy.17 = bf16[1,512,1024]{2,1,0:T(8,128)(2,1)} copy(bf16[1,512,1024]{2,1,0:T(8,128)(2,1)} %get-tuple-element.4) | data formatting | bytes 2097152
  98.7 1.4 %copy.18 = bf16[4,4,1024]{2,1,0:T(4,128)(2,1)} copy(bf16[4,4,1024]{2,1,0:T(4,128)(2,1)} %get-tuple-element.5) | data formatting | bytes 65536

commit v3 on v2

--- a/solution.py
+++ b/solution.py
@@ -23,7 +23,9 @@
 CAP = 16
 EXPERTS = 64
 GROUPS = 4
-FF_TILE = 512
+FF_TILE = 1024
+FIRST_SENT = 2
+SENT_AFTER = {0: (2,), 1: (3,)}
 
 
 def dot(a, b):
@@ -56,7 +58,7 @@
     tok, lat, clip, eid, slot, g1, g2, router, wqkv_hbm, wout_hbm, fin_hbm, fout_hbm,
     out, newb,
     wqkv, wout, fin, fout, latx, normed, packed, qmask, kmask, attended, mid, expert_in,
-    gate, disp, recv, outb, ret, acc, lat_send, lat_recv,
+    gate, disp, recv, outb, ret, hid, score, weight, act, lat_send, lat_recv,
     wsem, dsend, drecv, rsend, rrecv, lsem,
 ):
     m = lax.axis_index("mod")
@@ -160,10 +162,13 @@
         for half in range(2):
             mine = jnp.where(first if half == 0 else ~first, queries, jnp.zeros_like(queries))
             q = jnp.concatenate([mine, qmask[...]], axis=1)
-            s = dot_nt(q, keys)
-            top = jnp.max(s, axis=-1, keepdims=True)
-            w = jnp.exp(s - top).astype(BF16)
-            o = dot(w, values)
+            score[half] = dot_nt(q, keys)
+        for half in range(2):
+            for row0 in range(0, R, 48):
+                s = score[half, row0 : row0 + 48, :]
+                top = jnp.max(s, axis=-1, keepdims=True)
+                weight[half, row0 : row0 + 48, :] = jnp.exp(s - top).astype(BF16)
+            o = dot(weight[half], values)
             heads.append(o[:, :128] / o[:, 128:])
         attended[:, pl.ds(col, 128)] = jnp.where(first, heads[0], heads[1]).astype(BF16)
         return carry
@@ -198,12 +203,8 @@
         device_id=(1 - m, e), device_id_type=MESH,
     )
     lat_copy.start()
-    for g in range(GROUPS):
-        place = places(lax.broadcasted_iota(jnp.int32, (256, 1), 0), g)
-        onehot = jnp.where(place == pos_row, 1.0, 0.0).astype(BF16)
-        disp[g] = dot(onehot, expert_in[...]).astype(BF16).reshape(16, CAP, D)
-
-        def send(r, carry, g=g):
+    def dispatch(g):
+        def send(r, carry):
             j, there = partner(g, r, 1)
             pltpu.make_async_remote_copy(
                 src_ref=disp.at[g, j], dst_ref=recv.at[g, me],
@@ -213,9 +214,16 @@
             return carry
 
         lax.fori_loop(1 if g == 0 else 0, 16, send, 0)
+
+    for g in range(GROUPS):
+        place = places(lax.broadcasted_iota(jnp.int32, (256, 1), 0), g)
+        onehot = jnp.where(place == pos_row, 1.0, 0.0).astype(BF16)
+        disp[g] = dot(onehot, expert_in[...]).astype(BF16).reshape(16, CAP, D)
+        if g < FIRST_SENT:
+            dispatch(g)
     recv[0, me] = disp[0, me]
 
-    logits = dot(expert_in[...], router[...])
+    logits = dot_nt(expert_in[...], router[...])
     eid_col = column_of(eid[...].astype(F32)).astype(jnp.int32)
     expert_lane = lax.broadcasted_iota(jnp.int32, (T, EXPERTS), 1)
     picked = jnp.sum(jnp.where(expert_lane == eid_col, logits, 0.0), axis=1, keepdims=True)
@@ -228,18 +236,40 @@
         n = 15 if g == 0 else 16
         landed = recv.at[g, pl.ds(0, n)]
         pltpu.make_async_copy(landed, landed, drecv.at[g]).wait()
-        rows_in = recv[g].reshape(256, D)
-        acc[...] = jnp.zeros_like(acc)
-
-        def expert(f, carry, rows_in=rows_in):
-            cols = pl.ds(pl.multiple_of(f * FF_TILE, FF_TILE), FF_TILE)
-            h = dot(rows_in, fin[:, cols])
-            h = (0.5 * h * (1.0 + lax.erf(h * math.sqrt(0.5)))).astype(BF16)
-            acc[...] += dot(h, fout[cols, :])
-            return carry
-
-        lax.fori_loop(0, FF // FF_TILE, expert, 0)
-        outb[g] = acc[...].astype(BF16).reshape(16, CAP, D)
+        for later in SENT_AFTER.get(g, ()):
+            dispatch(later)
+
+        def activate(f, slot):
+            h = hid[slot]
+            h = 0.5 * h * (1.0 + lax.erf(h * math.sqrt(0.5)))
+            act[:, pl.ds(pl.multiple_of(f * FF_TILE, FF_TILE), FF_TILE)] = h.astype(BF16)
+
+        def first_layer(f, slot):
+            hid[slot] = dot(
+                recv[g].reshape(256, D),
+                fin[:, pl.ds(pl.multiple_of(f * FF_TILE, FF_TILE), FF_TILE)],
+            )
+
+        first_layer(0, 0)
+
+        def expert(i, carry):
+            first_layer(2 * i + 1, 1)
+            activate(2 * i, 0)
+            first_layer(2 * i + 2, 0)
+            activate(2 * i + 1, 1)
+            return carry
+
+        lax.fori_loop(0, FF // FF_TILE // 2 - 1, expert, 0)
+        first_layer(FF // FF_TILE - 1, 1)
+        activate(FF // FF_TILE - 2, 0)
+        activate(FF // FF_TILE - 1, 1)
+
+        def second_layer(f, carry, g=g):
+            cols = pl.ds(pl.multiple_of(f * 256, 256), 256)
+            outb[g, :, :, cols] = dot(act[...], fout[:, cols]).astype(BF16).reshape(16, CAP, 256)
+            return carry
+
+        lax.fori_loop(0, D // 256, second_layer, 0)
 
         def send_back(r, carry, g=g):
             j, there = partner(g, r, -1)
@@ -312,7 +342,10 @@
             pltpu.VMEM((GROUPS, 16, CAP, D), BF16),
             pltpu.VMEM((GROUPS, 16, CAP, D), BF16),
             pltpu.VMEM((GROUPS, 16, CAP, D), BF16),
-            pltpu.VMEM((256, D), F32),
+            pltpu.VMEM((2, 256, FF_TILE), F32),
+            pltpu.VMEM((2, R, KEYS), F32),
+            pltpu.VMEM((2, R, KEYS), BF16),
+            pltpu.VMEM((256, FF), BF16),
             pltpu.VMEM((L, D), BF16),
             pltpu.VMEM((L, D), BF16),
             dma((6,)),
@@ -326,7 +359,7 @@
             collective_id=0, has_side_effects=True, vmem_limit_bytes=62 * 2**20
         ),
     )(
-        tokens, bottleneck, clip_ids, expert_ids, slots, norm1_gain, norm2_gain, router,
+        tokens, bottleneck, clip_ids, expert_ids, slots, norm1_gain, norm2_gain, router.T,
         attn_qkv, attn_out, fc_in, fc_out,
     )
 

time: 100 us -> 91 us (0.910)
  the two profiles are of different devices: /device:TPU:1 before, /device:TPU:64 now
where the time goes in v3:
time: 91 us; the launch traced here: 90.8 us
  Pallas kernels  86.5 us (95%)
  local copies, waits for them, and re-layouts  3.65 us (4%)
    pallas_call x1, Pallas kernels, on_device(): pl.pallas_call(layer_kernel, out_shape=(jax.ShapeDtypeStruct(tokens.shape...  86.5 us
    unnamed x2, local copies, waits for them, and re-layouts  3.65 us

profile of v3, /device:TPU:64, one launch (start us, length us, event | category | flops | bytes accessed | tf_op | source)
XLA Modules:
  0.0 90.8 jit_solution(12680177375103800259)
XLA Ops:
  0.6 86.5 %shard_map.131 = (bf16[1,512,1024]{2,1,0:T(8,128)(2,1)}, bf16[4,4,1024]{2,1,0:T(4,128)(2,1)}) custom-call(bf16[1,512,1024]{2,1,0:T(8,128)(2,1)} %tok.1, bf16[4,4,1024]{2,1,0:T(4,128)(2,1)} %lat.1, s32[1,512]{1,0:T(1,128)} %clip.1, s32[1,512]{1,0:T(1,128)} %eid.1, s32[1,512]{1,0:T(1,128)} %slot.1, bf16[1,1024]{1,0:T(2,128)(2,1)} %g1.1, bf16[1,1024]{1,0:T(2,128)(2,1)} %g2.1, ...), custom_call_target="tpu_custom_call" | custom-call | tf_op jit(solution)/shard_map/pallas_call | solution.py:319
  87.1 2.3 %copy.16 = bf16[1,512,1024]{2,1,0:T(8,128)(2,1)} copy(bf16[1,512,1024]{2,1,0:T(8,128)(2,1)} %get-tuple-element.4) | data formatting | bytes 2097152
  89.4 1.4 %copy.17 = bf16[4,4,1024]{2,1,0:T(4,128)(2,1)} copy(bf16[4,4,1024]{2,1,0:T(4,128)(2,1)} %get-tuple-element.5) | data formatting | bytes 65536
